TPU v7x, 32 devices: a whole 2x2x4 slice. The times are simulated.
32 devices in a mesh: modes: 8 (over z, y), cheb: 4 (over x, core).
Axes of the slice: x: 2, y: 2, z: 4, core: 2. Of those that a mesh axis runs over, the one named last changes fastest.
Arguments:
- start: float32 [2, 2, 2048, 256], P(None, None, ('modes', 'cheb')), may hold values from -45 to 45
- forcing: float32 [2, 2, 2048, 256], P(None, None, ('modes', 'cheb')), may hold values from -45 to 45
- taus: float32 [2048, 256, 256], P(('modes', 'cheb')), may hold values from -5 to 5
Outputs:
- solution: float32 [2, 2, 2048, 256], P(None, None, ('modes', 'cheb'))
All inputs are finite; a program needn't handle non-finite values.
Results may differ from a plain program's by a relative error of at most 0.0002.
Values sent between devices are 32-bit elements; how exact they have to be, the bound alone decides.
A program may use at most 128 MiB of HBM per device.

v0:
```python
import math
import jax
import jax.numpy as jnp
from jax import lax
from jax.sharding import PartitionSpec as P

NEWTON = 2
KRYLOV = 3
HIGH = lax.Precision.HIGHEST
STRENGTH = 0.1


def cheb_rows(degree_count):
    degree = jnp.arange(degree_count, dtype=jnp.int32)[:, None]
    node = 2 * jnp.arange(degree_count, dtype=jnp.int32)[None, :] + 1
    turns = degree * node % (4 * degree_count)
    return jnp.cos(2.0 * math.pi / (4 * degree_count) * turns.astype(jnp.float32))


def phase_table(row_count, col_count, period):
    row_index = jnp.arange(row_count, dtype=jnp.int32)[:, None]
    col_index = jnp.arange(col_count, dtype=jnp.int32)[None, :]
    turns = row_index * col_index % period
    angle = 2.0 * math.pi / period * turns.astype(jnp.float32)
    return (jnp.cos(angle), jnp.sin(angle))


def inverse_points(spectrum, outer_len, inner_len, factor):
    half_inner = inner_len // 2
    lead_shape = spectrum.shape[:-3]
    row_count = spectrum.shape[-2]
    weights = jnp.where(jnp.arange(outer_len * half_inner) == 0, 1.0, 2.0).astype(jnp.float32)
    real_part = (spectrum[..., 0, :, :] * weights).reshape(
        lead_shape + (row_count, half_inner, outer_len)
    )
    imag_part = (spectrum[..., 1, :, :] * weights).reshape(
        lead_shape + (row_count, half_inner, outer_len)
    )
    section_cos, section_sin = phase_table(inner_len, half_inner, inner_len)
    upper_real = jnp.einsum(
        "jq,...yqa->...yja", section_cos, real_part, precision=HIGH
    ) - jnp.einsum("jq,...yqa->...yja", section_sin, imag_part, precision=HIGH)
    upper_imag = jnp.einsum(
        "jq,...yqa->...yja", section_sin, real_part, precision=HIGH
    ) + jnp.einsum("jq,...yqa->...yja", section_cos, imag_part, precision=HIGH)
    twist_cos, twist_sin = phase_table(inner_len, outer_len, inner_len * outer_len)
    turned_real = upper_real * twist_cos - upper_imag * twist_sin
    turned_imag = upper_real * twist_sin + upper_imag * twist_cos
    final_cos, final_sin = phase_table(outer_len, outer_len, outer_len)
    points = jnp.einsum("ta,...yja->...ytj", final_cos, turned_real, precision=HIGH) - jnp.einsum(
        "ta,...yja->...ytj", final_sin, turned_imag, precision=HIGH
    )
    return points.reshape(lead_shape + (row_count, outer_len * inner_len)) * factor


def forward_modes(points, outer_len, inner_len, factor):
    half_inner = inner_len // 2
    lead_shape = points.shape[:-2]
    row_count = points.shape[-2]
    gridded = points.reshape(lead_shape + (row_count, outer_len, inner_len))
    first_cos, first_sin = phase_table(outer_len, outer_len, outer_len)
    part_real = jnp.einsum("at,...ytj->...yaj", first_cos, gridded, precision=HIGH)
    part_imag = -jnp.einsum("at,...ytj->...yaj", first_sin, gridded, precision=HIGH)
    twist_cos, twist_sin = phase_table(outer_len, inner_len, inner_len * outer_len)
    turned_real = part_real * twist_cos + part_imag * twist_sin
    turned_imag = part_imag * twist_cos - part_real * twist_sin
    last_cos, last_sin = phase_table(half_inner, inner_len, inner_len)
    coef_real = jnp.einsum("qj,...yaj->...yqa", last_cos, turned_real, precision=HIGH) + jnp.einsum(
        "qj,...yaj->...yqa", last_sin, turned_imag, precision=HIGH
    )
    coef_imag = jnp.einsum("qj,...yaj->...yqa", last_cos, turned_imag, precision=HIGH) - jnp.einsum(
        "qj,...yaj->...yqa", last_sin, turned_real, precision=HIGH
    )
    coef_real = coef_real.reshape(lead_shape + (row_count, half_inner * outer_len))
    coef_imag = coef_imag.reshape(lead_shape + (row_count, half_inner * outer_len))
    return jnp.stack([coef_real, coef_imag], axis=-3) * factor


def least_squares(hessen, beta_norm):
    steps_count = len(hessen)
    matrix = [
        [hessen[col_index][:, row_index] for row_index in range(col_index + 2)]
        for col_index in range(steps_count)
    ]
    target = [beta_norm] + [jnp.zeros_like(beta_norm) for row_index in range(steps_count)]
    cosines = []
    sines_list = []
    for col_index in range(steps_count):
        column = matrix[col_index]
        for row_index in range(col_index):
            upper_entry = (
                cosines[row_index] * column[row_index]
                + sines_list[row_index] * column[row_index + 1]
            )
            lower_entry = (
                cosines[row_index] * column[row_index + 1]
                - sines_list[row_index] * column[row_index]
            )
            column[row_index] = upper_entry
            column[row_index + 1] = lower_entry
        radius = jnp.sqrt(
            column[col_index] * column[col_index] + column[col_index + 1] * column[col_index + 1]
        )
        cosines.append(column[col_index] / radius)
        sines_list.append(column[col_index + 1] / radius)
        column[col_index] = radius
        target[col_index + 1] = -sines_list[col_index] * target[col_index]
        target[col_index] = cosines[col_index] * target[col_index]
    solved = [None] * steps_count
    for row_index in reversed(range(steps_count)):
        partial_sum = target[row_index]
        for col_index in range(row_index + 1, steps_count):
            partial_sum = partial_sum - matrix[col_index][row_index] * solved[col_index]
        solved[row_index] = partial_sum / matrix[row_index][row_index]
    return solved


def shards(start, forcing, taus):
    group_size = lax.axis_size(("modes", "cheb"))
    local_modes = start.shape[2]
    degrees = start.shape[3]
    total_modes = local_modes * group_size
    points_count = 2 * total_modes
    outer_len = 2 ** ((points_count.bit_length() - 1) // 2)
    inner_len = points_count // outer_len
    spread = 1.0 / math.sqrt(total_modes * degrees)
    gather_factor = math.sqrt(total_modes * degrees) / points_count
    cheb_table = cheb_rows(degrees)
    offset = lax.axis_index(("modes", "cheb")) * local_modes
    wavenumber = (
        16.0 * (offset + jnp.arange(local_modes, dtype=jnp.int32)).astype(jnp.float32) / total_modes
    )
    tau_keep = (jnp.arange(degrees) < degrees - 2).astype(jnp.float32)
    coef_weights = jnp.where(jnp.arange(degrees) == 0, 1.0, 2.0).astype(jnp.float32) / degrees

    def move_out(stacked):
        return lax.all_to_all(stacked, ("modes", "cheb"), split_axis=3, concat_axis=4, tiled=True)

    def move_back(spectrum):
        return lax.all_to_all(spectrum, ("modes", "cheb"), split_axis=3, concat_axis=2, tiled=True)

    def to_points(coefs):
        values = jnp.einsum("brkn,ni->brik", coefs, cheb_table, precision=HIGH)
        slopes = jnp.stack([-wavenumber * values[:, 1], wavenumber * values[:, 0]], axis=1)
        spectrum = move_out(jnp.stack([values, slopes], axis=0))
        grid_pair = inverse_points(spectrum, outer_len, inner_len, spread)
        return (grid_pair[0], grid_pair[1])

    def to_coefficients(points):
        spectrum = forward_modes(points, outer_len, inner_len, gather_factor)
        slab_vals = move_back(spectrum)
        return jnp.einsum("brik,ni->brkn", slab_vals, cheb_table, precision=HIGH) * coef_weights

    def precondition(coefs):
        return jnp.einsum("kam,brkm->brka", taus, coefs * tau_keep, precision=HIGH)

    iterate = start
    for newton_step in range(NEWTON):
        base_points, base_slopes = to_points(iterate)
        residual = iterate + precondition(
            to_coefficients(STRENGTH * base_points * base_slopes) - forcing
        )
        squared = lax.psum(jnp.sum(residual * residual, axis=(1, 2, 3)), ("modes", "cheb"))
        beta_norm = jnp.sqrt(squared)
        krylov_basis = [-residual / beta_norm[:, None, None, None]]
        hessen = []
        for column in range(KRYLOV):
            probe_points, probe_slopes = to_points(krylov_basis[column])
            product = STRENGTH * (base_points * probe_slopes + probe_points * base_slopes)
            applied = krylov_basis[column] + precondition(to_coefficients(product))
            local_dots = jnp.stack(
                [jnp.sum(vector * applied, axis=(1, 2, 3)) for vector in krylov_basis], axis=1
            )
            local_square = jnp.sum(applied * applied, axis=(1, 2, 3))
            projections, square = lax.psum((local_dots, local_square), ("modes", "cheb"))
            remove_applied = applied
            for index, remove_vector in enumerate(krylov_basis):
                remove_applied = (
                    remove_applied - projections[:, index][:, None, None, None] * remove_vector
                )
            applied = remove_applied
            length = jnp.sqrt(square - jnp.sum(projections * projections, axis=1))
            hessen.append(jnp.concatenate([projections, length[:, None]], axis=1))
            krylov_basis.append(applied / length[:, None, None, None])
        solved = least_squares(hessen, beta_norm)
        for column in range(KRYLOV):
            iterate = iterate + solved[column][:, None, None, None] * krylov_basis[column]
    return iterate


def solution(mesh):
    return jax.shard_map(
        shards,
        mesh=mesh,
        in_specs=(
            P(None, None, ("modes", "cheb"), None),
            P(None, None, ("modes", "cheb"), None),
            P(("modes", "cheb"), None, None),
        ),
        out_specs=P(None, None, ("modes", "cheb"), None),
        check_vma=False,
    )
```

profile of v0, /device:TPU:0, one launch (start us, length us, event | category | flops | bytes accessed | tf_op | source)
XLA Modules:
  0.0 1151.1 jit_solution(514577233461936301)
XLA Ops:
  5.2 7.6 all-to-all-start
  13.3 14.9 %all-to-all-done = f32[32,1,4096]{2,1,0:T(1,128)S(1)} async-done(((f32[32,1,4096]{2,1,0:T(1,128)}), f32[32,1,4096]{2,1,0:T(1,128)S(1)}, u32[]{:S(2)}, u32[]{:S(2)}) %all-to-all-start) | async-done | bytes 524320 | tf_op jit(solution)/shard_map/all_to_all | solution.py:137
  48.1 4.3 copy.577
  52.4 7.9 reshape.338
  63.4 10.5 all-to-all-done.1
  75.2 7.6 reshape.339
  82.9 4.4 copy.769
  89.0 17.4 %fusion.14 = f32[64,2,2,256]{3,2,1,0:T(2,128)S(1)} fusion(f32[64,256,256]{2,1,0:T(8,128)} %param.5, f32[2,2,64,256]{3,2,1,0:T(8,128)S(1)} %fusion.73), kind=kOutput, calls=%fused_computation.14 | convolution fusion | flops 201326592 | bytes 17301504 | tf_op jit(solution)/shard_map/kam,brkm->brka/dot_general | solution.py:155
  106.6 38.5 %psum.98 = f32[2]{0:T(128)S(1)} all-reduce(f32[2]{0:T(128)S(1)} %multiply_reduce_fusion.19), channel_id=1, replica_groups=mesh['modes'=8,'cheb'=4] {'modes','cheb'}, use_global_device_ids=true, to_apply=%region_1.2 | all-reduce | flops 2 | bytes 16 | tf_op jit(solution)/shard_map/psum | solution.py:163
  148.7 19.1 %all_to_all.288 = f32[32,1,4096]{2,1,0:T(1,128)S(1)} all-to-all(f32[32,1,4096]{2,1,0:T(1,128)S(1)} %reshape.340), channel_id=1, replica_groups=mesh['modes'=8,'cheb'=4] {'modes','cheb'}, dimensions={0} | all-to-all | bytes 1048576 | tf_op jit(solution)/shard_map/all_to_all | solution.py:137
  191.7 4.3 copy.594
  196.1 7.2 reshape.342
  203.3 13.5 %all_to_all.289 = f32[32,1,2048]{2,1,0:T(1,128)S(1)} all-to-all(f32[32,1,2048]{2,1,0:T(1,128)S(1)} %reshape.342), channel_id=1, replica_groups=mesh['modes'=8,'cheb'=4] {'modes','cheb'}, dimensions={0} | all-to-all | bytes 524288 | tf_op jit(solution)/shard_map/all_to_all | solution.py:140
  218.0 7.6 reshape.343
  225.7 4.4 copy.771
  231.8 17.4 %fusion.12 = f32[64,2,2,256]{3,2,1,0:T(2,128)S(1)} fusion(f32[64,256,256]{2,1,0:T(8,128)} %param.5, f32[2,2,64,256]{3,2,1,0:T(8,128)S(1)} %fusion.74), kind=kOutput, calls=%fused_computation.12 | convolution fusion | flops 201326592 | bytes 17301504 | tf_op jit(solution)/shard_map/kam,brkm->brka/dot_general | solution.py:155
  249.4 38.6 %all-reduce.5 = (f32[2]{0:T(128)S(1)}, f32[2,1]{0,1:T(1,128)S(1)}) all-reduce(f32[2]{0:T(128)S(1)} %get-tuple-element.22, f32[2,1]{0,1:T(1,128)S(1)} %bitcast.1009), channel_id=1, replica_groups=mesh['modes'=8,'cheb'=4] {'modes','cheb'}, use_global_device_ids=true, to_apply=%region_5.6 | all-reduce | flops 4 | bytes 32 | tf_op jit(solution)/shard_map/psum | solution.py:175
  291.5 19.1 %all_to_all.290 = f32[32,1,4096]{2,1,0:T(1,128)S(1)} all-to-all(f32[32,1,4096]{2,1,0:T(1,128)S(1)} %reshape.344), channel_id=1, replica_groups=mesh['modes'=8,'cheb'=4] {'modes','cheb'}, dimensions={0} | all-to-all | bytes 1048576 | tf_op jit(solution)/shard_map/all_to_all | solution.py:137
  334.6 4.3 copy.611
  338.9 7.2 reshape.346
  346.1 13.5 %all_to_all.291 = f32[32,1,2048]{2,1,0:T(1,128)S(1)} all-to-all(f32[32,1,2048]{2,1,0:T(1,128)S(1)} %reshape.346), channel_id=1, replica_groups=mesh['modes'=8,'cheb'=4] {'modes','cheb'}, dimensions={0} | all-to-all | bytes 524288 | tf_op jit(solution)/shard_map/all_to_all | solution.py:140
  360.9 7.6 reshape.347
  368.5 4.4 copy.773
  374.7 17.4 %fusion.10 = f32[64,2,2,256]{3,2,1,0:T(2,128)S(1)} fusion(f32[64,256,256]{2,1,0:T(8,128)} %param.5, f32[2,2,64,256]{3,2,1,0:T(8,128)S(1)} %fusion.75), kind=kOutput, calls=%fused_computation.10 | convolution fusion | flops 201326592 | bytes 17301504 | tf_op jit(solution)/shard_map/kam,brkm->brka/dot_general | solution.py:155
  392.3 38.6 %all-reduce.4 = (f32[2]{0:T(128)S(1)}, f32[2,2]{0,1:T(2,128)S(1)}) all-reduce(f32[2]{0:T(128)S(1)} %get-tuple-element.19, f32[2,2]{0,1:T(2,128)S(1)} %pad_maximum_fusion.10), channel_id=1, replica_groups=mesh['modes'=8,'cheb'=4] {'modes','cheb'}, use_global_device_ids=true, to_apply=%region_10.11 | all-reduce | flops 6 | bytes 48 | tf_op jit(solution)/shard_map/psum | solution.py:175
  434.5 19.1 %all_to_all.292 = f32[32,1,4096]{2,1,0:T(1,128)S(1)} all-to-all(f32[32,1,4096]{2,1,0:T(1,128)S(1)} %reshape.348), channel_id=1, replica_groups=mesh['modes'=8,'cheb'=4] {'modes','cheb'}, dimensions={0} | all-to-all | bytes 1048576 | tf_op jit(solution)/shard_map/all_to_all | solution.py:137
  477.6 4.3 copy.628
  481.9 7.3 reshape.350
  489.2 13.5 %all_to_all.293 = f32[32,1,2048]{2,1,0:T(1,128)S(1)} all-to-all(f32[32,1,2048]{2,1,0:T(1,128)S(1)} %reshape.350), channel_id=1, replica_groups=mesh['modes'=8,'cheb'=4] {'modes','cheb'}, dimensions={0} | all-to-all | bytes 524288 | tf_op jit(solution)/shard_map/all_to_all | solution.py:140
  503.9 7.6 reshape.351
  511.6 4.4 copy.775
  517.7 17.4 %fusion.8 = f32[64,2,2,256]{3,2,1,0:T(2,128)S(1)} fusion(f32[64,256,256]{2,1,0:T(8,128)} %param.5, f32[2,2,64,256]{3,2,1,0:T(8,128)S(1)} %fusion.76), kind=kOutput, calls=%fused_computation.8 | convolution fusion | flops 201326592 | bytes 17301504 | tf_op jit(solution)/shard_map/kam,brkm->brka/dot_general | solution.py:155
  535.4 38.6 %all-reduce.3 = (f32[2]{0:T(128)S(1)}, f32[2,3]{0,1:T(4,128)S(1)}) all-reduce(f32[2]{0:T(128)S(1)} %get-tuple-element.16, f32[2,3]{0,1:T(4,128)S(1)} %pad_maximum_fusion.8), channel_id=1, replica_groups=mesh['modes'=8,'cheb'=4] {'modes','cheb'}, use_global_device_ids=true, to_apply=%region_17.18 | all-reduce | flops 8 | bytes 64 | tf_op jit(solution)/shard_map/psum | solution.py:175
  578.6 19.1 %all_to_all.294 = f32[32,1,4096]{2,1,0:T(1,128)S(1)} all-to-all(f32[32,1,4096]{2,1,0:T(1,128)S(1)} %reshape.352), channel_id=1, replica_groups=mesh['modes'=8,'cheb'=4] {'modes','cheb'}, dimensions={0} | all-to-all | bytes 1048576 | tf_op jit(solution)/shard_map/all_to_all | solution.py:137
  617.0 4.3 copy.645
  621.4 7.2 reshape.354
  628.6 13.5 %all_to_all.295 = f32[32,1,2048]{2,1,0:T(1,128)S(1)} all-to-all(f32[32,1,2048]{2,1,0:T(1,128)S(1)} %reshape.354), channel_id=1, replica_groups=mesh['modes'=8,'cheb'=4] {'modes','cheb'}, dimensions={0} | all-to-all | bytes 524288 | tf_op jit(solution)/shard_map/all_to_all | solution.py:140
  643.3 7.6 reshape.355
  651.0 4.4 copy.777
  657.1 17.4 %fusion.6 = f32[64,2,2,256]{3,2,1,0:T(2,128)S(1)} fusion(f32[64,256,256]{2,1,0:T(8,128)} %param.5, f32[2,2,64,256]{3,2,1,0:T(8,128)S(1)} %fusion.78), kind=kOutput, calls=%fused_computation.6 | convolution fusion | flops 201326592 | bytes 17301504 | tf_op jit(solution)/shard_map/kam,brkm->brka/dot_general | solution.py:155
  674.7 38.5 %psum.105 = f32[2]{0:T(128)S(1)} all-reduce(f32[2]{0:T(128)S(1)} %multiply_reduce_fusion.9), channel_id=1, replica_groups=mesh['modes'=8,'cheb'=4] {'modes','cheb'}, use_global_device_ids=true, to_apply=%region_20.21 | all-reduce | flops 2 | bytes 16 | tf_op jit(solution)/shard_map/psum | solution.py:163
  716.8 19.1 %all_to_all.296 = f32[32,1,4096]{2,1,0:T(1,128)S(1)} all-to-all(f32[32,1,4096]{2,1,0:T(1,128)S(1)} %reshape.356), channel_id=1, replica_groups=mesh['modes'=8,'cheb'=4] {'modes','cheb'}, dimensions={0} | all-to-all | bytes 1048576 | tf_op jit(solution)/shard_map/all_to_all | solution.py:137
  759.8 4.3 copy.662
  764.2 7.2 reshape.358
  771.4 13.5 %all_to_all.297 = f32[32,1,2048]{2,1,0:T(1,128)S(1)} all-to-all(f32[32,1,2048]{2,1,0:T(1,128)S(1)} %reshape.358), channel_id=1, replica_groups=mesh['modes'=8,'cheb'=4] {'modes','cheb'}, dimensions={0} | all-to-all | bytes 524288 | tf_op jit(solution)/shard_map/all_to_all | solution.py:140
  786.1 7.6 reshape.359
  793.8 4.4 copy.779
  799.9 17.4 %fusion.4 = f32[64,2,2,256]{3,2,1,0:T(2,128)S(1)} fusion(f32[64,256,256]{2,1,0:T(8,128)} %param.5, f32[2,2,64,256]{3,2,1,0:T(8,128)S(1)} %fusion.79), kind=kOutput, calls=%fused_computation.4 | convolution fusion | flops 201326592 | bytes 17301504 | tf_op jit(solution)/shard_map/kam,brkm->brka/dot_general | solution.py:155
  817.5 38.6 %all-reduce.2 = (f32[2]{0:T(128)S(1)}, f32[2,1]{0,1:T(1,128)S(1)}) all-reduce(f32[2]{0:T(128)S(1)} %get-tuple-element.13, f32[2,1]{0,1:T(1,128)S(1)} %bitcast.1010), channel_id=1, replica_groups=mesh['modes'=8,'cheb'=4] {'modes','cheb'}, use_global_device_ids=true, to_apply=%region_24.25 | all-reduce | flops 4 | bytes 32 | tf_op jit(solution)/shard_map/psum | solution.py:175
  859.6 19.1 %all_to_all.298 = f32[32,1,4096]{2,1,0:T(1,128)S(1)} all-to-all(f32[32,1,4096]{2,1,0:T(1,128)S(1)} %reshape.360), channel_id=1, replica_groups=mesh['modes'=8,'cheb'=4] {'modes','cheb'}, dimensions={0} | all-to-all | bytes 1048576 | tf_op jit(solution)/shard_map/all_to_all | solution.py:137
  904.3 4.3 copy.679
  908.6 7.2 reshape.362
  915.8 13.5 %all_to_all.299 = f32[32,1,2048]{2,1,0:T(1,128)S(1)} all-to-all(f32[32,1,2048]{2,1,0:T(1,128)S(1)} %reshape.362), channel_id=1, replica_groups=mesh['modes'=8,'cheb'=4] {'modes','cheb'}, dimensions={0} | all-to-all | bytes 524288 | tf_op jit(solution)/shard_map/all_to_all | solution.py:140
  930.6 7.6 reshape.363
  938.2 4.4 copy.781
  944.4 17.4 %fusion.2 = f32[64,2,2,256]{3,2,1,0:T(2,128)S(1)} fusion(f32[64,256,256]{2,1,0:T(8,128)} %param.5, f32[2,2,64,256]{3,2,1,0:T(8,128)S(1)} %fusion.80), kind=kOutput, calls=%fused_computation.2 | convolution fusion | flops 201326592 | bytes 17301504 | tf_op jit(solution)/shard_map/kam,brkm->brka/dot_general | solution.py:155
  962.0 38.6 %all-reduce.1 = (f32[2]{0:T(128)S(1)}, f32[2,2]{0,1:T(2,128)S(1)}) all-reduce(f32[2]{0:T(128)S(1)} %get-tuple-element.10, f32[2,2]{0,1:T(2,128)S(1)} %pad_maximum_fusion.11), channel_id=1, replica_groups=mesh['modes'=8,'cheb'=4] {'modes','cheb'}, use_global_device_ids=true, to_apply=%region_29.30 | all-reduce | flops 6 | bytes 48 | tf_op jit(solution)/shard_map/psum | solution.py:175
  1006.7 19.3 %all_to_all.300 = f32[32,1,4096]{2,1,0:T(1,128)S(1)} all-to-all(f32[32,1,4096]{2,1,0:T(1,128)} %reshape.364), channel_id=1, replica_groups=mesh['modes'=8,'cheb'=4] {'modes','cheb'}, dimensions={0} | all-to-all | bytes 1048576 | tf_op jit(solution)/shard_map/all_to_all | solution.py:137
  1058.0 7.3 reshape.366
  1065.2 13.5 %all_to_all.301 = f32[32,1,2048]{2,1,0:T(1,128)S(1)} all-to-all(f32[32,1,2048]{2,1,0:T(1,128)S(1)} %reshape.366), channel_id=1, replica_groups=mesh['modes'=8,'cheb'=4] {'modes','cheb'}, dimensions={0} | all-to-all | bytes 524288 | tf_op jit(solution)/shard_map/all_to_all | solution.py:140
  1080.0 7.6 reshape.367
  1087.6 4.4 copy.783
  1093.8 17.4 %fusion = f32[64,2,2,256]{3,2,1,0:T(2,128)S(1)} fusion(f32[64,256,256]{2,1,0:T(8,128)} %param.5, f32[2,2,64,256]{3,2,1,0:T(8,128)S(1)} %fusion.81), kind=kOutput, calls=%fused_computation | convolution fusion | flops 201326592 | bytes 17301504 | tf_op jit(solution)/shard_map/kam,brkm->brka/dot_general | solution.py:155
  1111.4 38.6 %all-reduce = (f32[2]{0:T(128)S(1)}, f32[2,3]{0,1:T(4,128)S(1)}) all-reduce(f32[2]{0:T(128)S(1)} %get-tuple-element.7, f32[2,3]{0,1:T(4,128)S(1)} %pad_maximum_fusion.9), channel_id=1, replica_groups=mesh['modes'=8,'cheb'=4] {'modes','cheb'}, use_global_device_ids=true, to_apply=%region_36.37 | all-reduce | flops 8 | bytes 64 | tf_op jit(solution)/shard_map/psum | solution.py:175
  (316 shorter events, 254.3 us)
Async XLA Ops:
  5.2 23.0 %all-to-all-start = ((f32[32,1,4096]{2,1,0:T(1,128)}), f32[32,1,4096]{2,1,0:T(1,128)S(1)}, u32[]{:S(2)}, u32[]{:S(2)}) async-start(f32[32,1,4096]{2,1,0:T(1,128)} %reshape.336), calls=%async_computation | async-start | bytes 1048576 | tf_op jit(solution)/shard_map/all_to_all | solution.py:137
  42.3 45.0 %copy-start.5 = (f32[2,2,64,256]{3,2,1,0:T(8,128)S(1)}, f32[2,2,64,256]{3,2,1,0:T(8,128)}, u32[]{:S(2)}) copy-start(f32[2,2,64,256]{3,2,1,0:T(8,128)} %param.4) | copy-start | bytes 786436
  52.4 54.0 %copy-start = (f32[2,2,64,256]{3,2,1,0:T(8,128)S(1)}, f32[2,2,64,256]{3,2,1,0:T(8,128)}, u32[]{:S(2)}) copy-start(f32[2,2,64,256]{3,2,1,0:T(8,128)} %param.3) | copy-start | bytes 786436
  60.3 13.7 %all-to-all-start.1 = ((f32[32,1,2048]{2,1,0:T(1,128)}), f32[32,1,2048]{2,1,0:T(1,128)S(1)}, u32[]{:S(2)}, u32[]{:S(2)}) async-start(f32[32,1,2048]{2,1,0:T(1,128)} %reshape.338), calls=%async_computation.1 | async-start | bytes 524288 | tf_op jit(solution)/shard_map/all_to_all | solution.py:140
  431.1 104.0 %copy-start.4 = (f32[2,2,64,256]{3,2,1,0:T(8,128)}, f32[2,2,64,256]{3,2,1,0:T(8,128)S(1)}, u32[]{:S(2)}) copy-start(f32[2,2,64,256]{3,2,1,0:T(8,128)S(1)} %subtract_divide_fusion.2) | copy-start | bytes 786436
  481.9 92.2 %copy-start.1 = (f32[2,2,64,256]{3,2,1,0:T(8,128)S(1)}, f32[2,2,64,256]{3,2,1,0:T(8,128)}, u32[]{:S(2)}) copy-start(f32[2,2,64,256]{3,2,1,0:T(8,128)} %param.3) | copy-start | bytes 786436
  611.3 44.1 %copy-start.6 = (f32[2,2,64,256]{3,2,1,0:T(8,128)S(1)}, f32[2,2,64,256]{3,2,1,0:T(8,128)}, u32[]{:S(2)}) copy-start(f32[2,2,64,256]{3,2,1,0:T(8,128)} %param.4) | copy-start | bytes 786436
  1000.8 38.3 %copy-start.2 = (f32[2,2,64,256]{3,2,1,0:T(8,128)}, f32[2,2,64,256]{3,2,1,0:T(8,128)S(1)}, u32[]{:S(2)}) copy-start(f32[2,2,64,256]{3,2,1,0:T(8,128)S(1)} %subtract_divide_fusion) | copy-start | bytes 786436
  1058.0 53.2 %copy-start.3 = (f32[2,2,64,256]{3,2,1,0:T(8,128)S(1)}, f32[2,2,64,256]{3,2,1,0:T(8,128)}, u32[]{:S(2)}) copy-start(f32[2,2,64,256]{3,2,1,0:T(8,128)} %copy-done.2) | copy-start | bytes 786436
where the time goes:
time: 1160 us; the launch traced here: 1150 us
  blocking collectives  537 us (46%)
  matrix products  312 us (27%)
  local copies, waits for them, and re-layouts  229 us (20%)
  other arithmetic  34.4 us (3%)
  waiting for transfers between devices  25.4 us (2%)
    psum x6, blocking collectives, shards(): lax.psum((local_dots, local_square), ('modes', 'cheb'))  232 us
    dot_general x8, matrix products, precondition(): return jnp.einsum('kam,brkm->brka', taus, coefs * tau_keep, precision=HIGH)  139 us
    unnamed x46, local copies, waits for them, and re-layouts  137 us
    all_to_all x7, blocking collectives, move_out(): lax.all_to_all(stacked, ('modes', 'cheb'), split_axis=3, concat_axis=4, t...  134 us
    all_to_all x7, blocking collectives, move_back(): lax.all_to_all(spectrum, ('modes', 'cheb'), split_axis=3, concat_axis=2,...  94.6 us
    psum x2, blocking collectives, shards(): lax.psum(jnp.sum(residual * residual, axis=(1, 2, 3)), ('modes', 'cheb'))  77.1 us
    all_to_all x8, local copies, waits for them, and re-layouts, move_back(): lax.all_to_all(spectrum, ('modes', 'cheb'), split_axis=3, concat_axis=2,...  35.3 us
    mul x8, local copies, waits for them, and re-layouts, forward_modes(): return jnp.stack([coef_real, coef_imag], axis=-3) * factor  34.5 us
  transfers between devices with their start and end apart: 2, of which 2 were waited for; matrix products, arithmetic and copies ran while one was open for 0% of the time, Pallas kernels for 0%

commit v1 on v0

--- a/solution.py
+++ b/solution.py
@@ -3,6 +3,7 @@
 import jax.numpy as jnp
 from jax import lax
 from jax.sharding import PartitionSpec as P
+from jax.lax import all_to_all, psum
 
 NEWTON = 2
 KRYLOV = 3
@@ -134,7 +135,19 @@
     coef_weights = jnp.where(jnp.arange(degrees) == 0, 1.0, 2.0).astype(jnp.float32) / degrees
 
     def move_out(stacked):
-        return lax.all_to_all(stacked, ("modes", "cheb"), split_axis=3, concat_axis=4, tiled=True)
+
+        def fix_grid(x0, lane_axis):
+            return jnp.concatenate(
+                all_to_all(
+                    jnp.stack(jnp.split(x0, psum(1, axis_name=lane_axis), 3), axis=0),
+                    axis_name=lane_axis,
+                    split_axis=0,
+                    concat_axis=0,
+                ),
+                4,
+            )
+
+        return fix_grid(stacked, ("modes", "cheb"))
 
     def move_back(spectrum):
         return lax.all_to_all(spectrum, ("modes", "cheb"), split_axis=3, concat_axis=2, tiled=True)

time: 1160 us -> 1540 us (1.33)
  local copies, waits for them, and re-layouts: 229 us -> 553 us
  other arithmetic: 34.4 us -> 81.6 us
    another operation x8 -> x264, local copies, waits for them, and re-layouts: 7.04 us -> 253 us  [fix_grid(): jnp.stack(jnp.split(x0, psum(1, axis_name=lane_axis), 3), axis=0)]
    unnamed x46 -> x374, local copies, waits for them, and re-layouts: 137 us -> 208 us
    another operation x0 -> x32, other arithmetic: none -> 50.7 us  [fix_grid(): jnp.stack(jnp.split(x0, psum(1, axis_name=lane_axis), 3), axis=0)]
    reshape x0 -> x16, local copies, waits for them, and re-layouts: none -> 16.6 us  [fix_grid(): jnp.concatenate(all_to_all(jnp.stack(jnp.split(x0, psum(1, axis_name=lane...]
where the time goes in v1:
time: 1540 us; the launch traced here: 1530 us
  local copies, waits for them, and re-layouts  553 us (36%)
  blocking collectives  539 us (35%)
  matrix products  311 us (20%)
  other arithmetic  81.6 us (5%)
  waiting for transfers between devices  25.5 us (2%)
    another operation x264, local copies, waits for them, and re-layouts, fix_grid(): jnp.stack(jnp.split(x0, psum(1, axis_name=lane_axis), 3), axis=0)  253 us
    psum x6, blocking collectives, shards(): lax.psum((local_dots, local_square), ('modes', 'cheb'))  233 us
    unnamed x374, local copies, waits for them, and re-layouts  208 us
    dot_general x8, matrix products, precondition(): return jnp.einsum('kam,brkm->brka', taus, coefs * tau_keep, precision=HIGH)  139 us
    all_to_all x7, blocking collectives, fix_grid(): all_to_all(jnp.stack(jnp.split(x0, psum(1, axis_name=lane_axis), 3), axis...  134 us
    all_to_all x7, blocking collectives, move_back(): lax.all_to_all(spectrum, ('modes', 'cheb'), split_axis=3, concat_axis=2,...  95.2 us
    psum x2, blocking collectives, shards(): lax.psum(jnp.sum(residual * residual, axis=(1, 2, 3)), ('modes', 'cheb'))  77.5 us
    another operation x32, other arithmetic, fix_grid(): jnp.stack(jnp.split(x0, psum(1, axis_name=lane_axis), 3), axis=0)  50.7 us
  transfers between devices with their start and end apart: 2, of which 2 were waited for; matrix products, arithmetic and copies ran while one was open for 0% of the time, Pallas kernels for 0%

profile of v1, /device:TPU:0, one launch (start us, length us, event | category | flops | bytes accessed | tf_op | source)
XLA Modules:
  0.0 1525.5 jit_solution(14764241050535626817)
XLA Ops:
  48.0 7.5 all-to-all-start
  56.0 15.0 all-to-all-done
  90.6 4.3 copy.1071
  94.9 7.9 reshape.402
  106.2 10.5 all-to-all-done.1
  118.0 7.6 reshape.403
  125.6 4.4 copy.1473
  131.8 17.4 %fusion.14 = f32[64,2,2,256]{3,2,1,0:T(2,128)S(1)} fusion(f32[64,256,256]{2,1,0:T(8,128)} %param.5, f32[2,2,64,256]{3,2,1,0:T(8,128)S(1)} %fusion.73), kind=kOutput, calls=%fused_computation.14 | convolution fusion | flops 201326592 | bytes 17301504 | tf_op jit(solution)/shard_map/kam,brkm->brka/dot_general | solution.py:168
  149.4 38.7 %psum.98 = f32[2]{0:T(128)S(1)} all-reduce(f32[2]{0:T(128)S(1)} %multiply_reduce_fusion.19), channel_id=1, replica_groups=mesh['modes'=8,'cheb'=4] {'modes','cheb'}, use_global_device_ids=true, to_apply=%region_1.2 | all-reduce | flops 2 | bytes 16 | tf_op jit(solution)/shard_map/psum | solution.py:176
  225.6 19.1 %all_to_all.184 = f32[32,1,4096]{2,1,0:T(1,128)S(1)} all-to-all(f32[32,1,4096]{2,1,0:T(1,128)S(1)} %reshape.404), channel_id=1, replica_groups=mesh['modes'=8,'cheb'=4] {'modes','cheb'}, dimensions={0} | all-to-all | bytes 1048576 | tf_op jit(solution)/shard_map/all_to_all | solution.py:141
  268.5 4.3 copy.1118
  272.8 7.2 reshape.406
  280.0 13.5 all_to_all.185
  294.8 7.6 reshape.407
  302.5 4.4 copy.1475
  308.6 17.4 %fusion.12 = f32[64,2,2,256]{3,2,1,0:T(2,128)S(1)} fusion(f32[64,256,256]{2,1,0:T(8,128)} %param.5, f32[2,2,64,256]{3,2,1,0:T(8,128)S(1)} %fusion.74), kind=kOutput, calls=%fused_computation.12 | convolution fusion | flops 201326592 | bytes 17301504 | tf_op jit(solution)/shard_map/kam,brkm->brka/dot_general | solution.py:168
  326.2 38.8 %all-reduce.5 = (f32[2]{0:T(128)S(1)}, f32[2,1]{0,1:T(1,128)S(1)}) all-reduce(f32[2]{0:T(128)S(1)} %get-tuple-element.22, f32[2,1]{0,1:T(1,128)S(1)} %bitcast.1481), channel_id=1, replica_groups=mesh['modes'=8,'cheb'=4] {'modes','cheb'}, use_global_device_ids=true, to_apply=%region_5.6 | all-reduce | flops 4 | bytes 32 | tf_op jit(solution)/shard_map/psum | solution.py:188
  423.7 19.1 %all_to_all.186 = f32[32,1,4096]{2,1,0:T(1,128)S(1)} all-to-all(f32[32,1,4096]{2,1,0:T(1,128)S(1)} %reshape.408), channel_id=1, replica_groups=mesh['modes'=8,'cheb'=4] {'modes','cheb'}, dimensions={0} | all-to-all | bytes 1048576 | tf_op jit(solution)/shard_map/all_to_all | solution.py:141
  468.6 4.3 copy.1165
  472.9 7.2 reshape.410
  480.2 13.6 all_to_all.187
  495.0 7.6 reshape.411
  502.6 4.4 copy.1477
  508.8 17.4 %fusion.10 = f32[64,2,2,256]{3,2,1,0:T(2,128)S(1)} fusion(f32[64,256,256]{2,1,0:T(8,128)} %param.5, f32[2,2,64,256]{3,2,1,0:T(8,128)S(1)} %fusion.75), kind=kOutput, calls=%fused_computation.10 | convolution fusion | flops 201326592 | bytes 17301504 | tf_op jit(solution)/shard_map/kam,brkm->brka/dot_general | solution.py:168
  526.4 39.0 %all-reduce.4 = (f32[2]{0:T(128)S(1)}, f32[2,2]{0,1:T(2,128)S(1)}) all-reduce(f32[2]{0:T(128)S(1)} %get-tuple-element.19, f32[2,2]{0,1:T(2,128)S(1)} %pad_maximum_fusion.10), channel_id=1, replica_groups=mesh['modes'=8,'cheb'=4] {'modes','cheb'}, use_global_device_ids=true, to_apply=%region_10.11 | all-reduce | flops 6 | bytes 48 | tf_op jit(solution)/shard_map/psum | solution.py:188
  623.2 19.1 %all_to_all.188 = f32[32,1,4096]{2,1,0:T(1,128)S(1)} all-to-all(f32[32,1,4096]{2,1,0:T(1,128)S(1)} %reshape.412), channel_id=1, replica_groups=mesh['modes'=8,'cheb'=4] {'modes','cheb'}, dimensions={0} | all-to-all | bytes 1048576 | tf_op jit(solution)/shard_map/all_to_all | solution.py:141
  668.2 4.3 copy.1212
  672.6 7.3 reshape.414
  679.9 13.8 all_to_all.189
  694.9 7.6 reshape.415
  702.5 4.4 copy.1479
  708.7 17.4 %fusion.8 = f32[64,2,2,256]{3,2,1,0:T(2,128)S(1)} fusion(f32[64,256,256]{2,1,0:T(8,128)} %param.5, f32[2,2,64,256]{3,2,1,0:T(8,128)S(1)} %fusion.76), kind=kOutput, calls=%fused_computation.8 | convolution fusion | flops 201326592 | bytes 17301504 | tf_op jit(solution)/shard_map/kam,brkm->brka/dot_general | solution.py:168
  726.3 38.8 %all-reduce.3 = (f32[2]{0:T(128)S(1)}, f32[2,3]{0,1:T(4,128)S(1)}) all-reduce(f32[2]{0:T(128)S(1)} %get-tuple-element.16, f32[2,3]{0,1:T(4,128)S(1)} %pad_maximum_fusion.8), channel_id=1, replica_groups=mesh['modes'=8,'cheb'=4] {'modes','cheb'}, use_global_device_ids=true, to_apply=%region_17.18 | all-reduce | flops 8 | bytes 64 | tf_op jit(solution)/shard_map/psum | solution.py:188
  812.8 19.1 %all_to_all.190 = f32[32,1,4096]{2,1,0:T(1,128)S(1)} all-to-all(f32[32,1,4096]{2,1,0:T(1,128)S(1)} %reshape.416), channel_id=1, replica_groups=mesh['modes'=8,'cheb'=4] {'modes','cheb'}, dimensions={0} | all-to-all | bytes 1048576 | tf_op jit(solution)/shard_map/all_to_all | solution.py:141
  851.1 4.3 copy.1259
  855.4 7.2 reshape.418
  862.6 13.5 all_to_all.191
  877.4 7.6 reshape.419
  885.1 4.4 copy.1481
  891.3 17.4 %fusion.6 = f32[64,2,2,256]{3,2,1,0:T(2,128)S(1)} fusion(f32[64,256,256]{2,1,0:T(8,128)} %param.5, f32[2,2,64,256]{3,2,1,0:T(8,128)S(1)} %fusion.78), kind=kOutput, calls=%fused_computation.6 | convolution fusion | flops 201326592 | bytes 17301504 | tf_op jit(solution)/shard_map/kam,brkm->brka/dot_general | solution.py:168
  908.8 38.7 %psum.105 = f32[2]{0:T(128)S(1)} all-reduce(f32[2]{0:T(128)S(1)} %multiply_reduce_fusion.9), channel_id=1, replica_groups=mesh['modes'=8,'cheb'=4] {'modes','cheb'}, use_global_device_ids=true, to_apply=%region_20.21 | all-reduce | flops 2 | bytes 16 | tf_op jit(solution)/shard_map/psum | solution.py:176
  985.1 19.1 %all_to_all.192 = f32[32,1,4096]{2,1,0:T(1,128)S(1)} all-to-all(f32[32,1,4096]{2,1,0:T(1,128)S(1)} %reshape.420), channel_id=1, replica_groups=mesh['modes'=8,'cheb'=4] {'modes','cheb'}, dimensions={0} | all-to-all | bytes 1048576 | tf_op jit(solution)/shard_map/all_to_all | solution.py:141
  1032.1 7.2 reshape.422
  1039.3 13.6 all_to_all.193
  1054.1 7.6 reshape.423
  1061.8 4.4 copy.1483
  1067.9 17.4 %fusion.4 = f32[64,2,2,256]{3,2,1,0:T(2,128)S(1)} fusion(f32[64,256,256]{2,1,0:T(8,128)} %param.5, f32[2,2,64,256]{3,2,1,0:T(8,128)S(1)} %fusion.79), kind=kOutput, calls=%fused_computation.4 | convolution fusion | flops 201326592 | bytes 17301504 | tf_op jit(solution)/shard_map/kam,brkm->brka/dot_general | solution.py:168
  1085.5 39.0 %all-reduce.2 = (f32[2]{0:T(128)S(1)}, f32[2,1]{0,1:T(1,128)S(1)}) all-reduce(f32[2]{0:T(128)S(1)} %get-tuple-element.13, f32[2,1]{0,1:T(1,128)S(1)} %bitcast.1482), channel_id=1, replica_groups=mesh['modes'=8,'cheb'=4] {'modes','cheb'}, use_global_device_ids=true, to_apply=%region_24.25 | all-reduce | flops 4 | bytes 32 | tf_op jit(solution)/shard_map/psum | solution.py:188
  1183.2 19.1 %all_to_all.194 = f32[32,1,4096]{2,1,0:T(1,128)S(1)} all-to-all(f32[32,1,4096]{2,1,0:T(1,128)S(1)} %reshape.424), channel_id=1, replica_groups=mesh['modes'=8,'cheb'=4] {'modes','cheb'}, dimensions={0} | all-to-all | bytes 1048576 | tf_op jit(solution)/shard_map/all_to_all | solution.py:141
  1228.2 4.3 copy.1353
  1232.5 7.2 reshape.426
  1239.7 13.8 all_to_all.195
  1254.7 7.6 reshape.427
  1262.4 4.4 copy.1485
  1268.5 17.4 %fusion.2 = f32[64,2,2,256]{3,2,1,0:T(2,128)S(1)} fusion(f32[64,256,256]{2,1,0:T(8,128)} %param.5, f32[2,2,64,256]{3,2,1,0:T(8,128)S(1)} %fusion.80), kind=kOutput, calls=%fused_computation.2 | convolution fusion | flops 201326592 | bytes 17301504 | tf_op jit(solution)/shard_map/kam,brkm->brka/dot_general | solution.py:168
  1286.1 38.8 %all-reduce.1 = (f32[2]{0:T(128)S(1)}, f32[2,2]{0,1:T(2,128)S(1)}) all-reduce(f32[2]{0:T(128)S(1)} %get-tuple-element.10, f32[2,2]{0,1:T(2,128)S(1)} %pad_maximum_fusion.11), channel_id=1, replica_groups=mesh['modes'=8,'cheb'=4] {'modes','cheb'}, use_global_device_ids=true, to_apply=%region_29.30 | all-reduce | flops 6 | bytes 48 | tf_op jit(solution)/shard_map/psum | solution.py:188
  1382.7 19.1 %all_to_all.196 = f32[32,1,4096]{2,1,0:T(1,128)S(1)} all-to-all(f32[32,1,4096]{2,1,0:T(1,128)S(1)} %reshape.428), channel_id=1, replica_groups=mesh['modes'=8,'cheb'=4] {'modes','cheb'}, dimensions={0} | all-to-all | bytes 1048576 | tf_op jit(solution)/shard_map/all_to_all | solution.py:141
  1427.8 4.3 copy.1400
  1432.2 7.3 reshape.430
  1439.5 13.5 all_to_all.197
  1454.2 7.6 reshape.431
  1461.9 4.4 copy.1487
  1468.1 17.4 %fusion = f32[64,2,2,256]{3,2,1,0:T(2,128)S(1)} fusion(f32[64,256,256]{2,1,0:T(8,128)} %param.5, f32[2,2,64,256]{3,2,1,0:T(8,128)S(1)} %fusion.81), kind=kOutput, calls=%fused_computation | convolution fusion | flops 201326592 | bytes 17301504 | tf_op jit(solution)/shard_map/kam,brkm->brka/dot_general | solution.py:168
  1485.7 38.6 %all-reduce = (f32[2]{0:T(128)S(1)}, f32[2,3]{0,1:T(4,128)S(1)}) all-reduce(f32[2]{0:T(128)S(1)} %get-tuple-element.7, f32[2,3]{0,1:T(4,128)S(1)} %pad_maximum_fusion.9), channel_id=1, replica_groups=mesh['modes'=8,'cheb'=4] {'modes','cheb'}, use_global_device_ids=true, to_apply=%region_36.37 | all-reduce | flops 8 | bytes 64 | tf_op jit(solution)/shard_map/psum | solution.py:188
  (916 shorter events, 625.0 us)
Async XLA Ops:
  0.0 8.1 copy-start.34
  0.0 8.1 copy-start.4
  0.0 8.1 copy-start.8
  48.0 22.9 %all-to-all-start = ((f32[32,1,4096]{2,1,0:T(1,128)}), f32[32,1,4096]{2,1,0:T(1,128)S(1)}, u32[]{:S(2)}, u32[]{:S(2)}) async-start(f32[32,1,4096]{2,1,0:T(1,128)} %reshape.400), calls=%async_computation | async-start | bytes 1048576 | tf_op jit(solution)/shard_map/all_to_all | solution.py:141
  84.8 45.3 %copy-start.32 = (f32[2,2,64,256]{3,2,1,0:T(8,128)S(1)}, f32[2,2,64,256]{3,2,1,0:T(8,128)}, u32[]{:S(2)}) copy-start(f32[2,2,64,256]{3,2,1,0:T(8,128)} %param.4) | copy-start | bytes 786436
  84.8 45.3 %copy-start.35 = (s32[256]{0:T(256)S(1)}, s32[256]{0:T(256)}, u32[]{:S(2)}) copy-start(s32[256]{0:T(256)} %copy-done.34) | copy-start | bytes 3076
  94.9 54.3 %copy-start.2 = (f32[2,2,64,256]{3,2,1,0:T(8,128)S(1)}, f32[2,2,64,256]{3,2,1,0:T(8,128)}, u32[]{:S(2)}) copy-start(f32[2,2,64,256]{3,2,1,0:T(8,128)} %param.3) | copy-start | bytes 786436
  94.9 94.7 %copy-start.5 = (f32[64]{0:T(128)S(1)}, f32[64]{0:T(128)}, u32[]{:S(2)}) copy-start(f32[64]{0:T(128)} %copy-done.4) | copy-start | bytes 772
  94.9 94.7 %copy-start.9 = (f32[64]{0:T(128)S(1)}, f32[64]{0:T(128)}, u32[]{:S(2)}) copy-start(f32[64]{0:T(128)} %copy-done.8) | copy-start | bytes 772
  102.8 14.0 all-to-all-start.1
  106.2 400.9 %copy-start.39 = (f32[256]{0:T(256)}, f32[256]{0:T(256)S(1)}, u32[]{:S(2)}) copy-start(f32[256]{0:T(256)S(1)} %fusion.1144) | copy-start | bytes 3076
  106.2 400.9 %copy-start.43 = (f32[256]{0:T(256)}, f32[256]{0:T(256)S(1)}, u32[]{:S(2)}) copy-start(f32[256]{0:T(256)S(1)} %compare_convert_fusion) | copy-start | bytes 3076
  188.1 1.5 copy-start.30
  365.0 1.6 copy-start.14
  365.0 1.6 copy-start.26
  565.4 1.7 copy-start.18
  565.5 1.7 copy-start.22
  662.2 44.7 %copy-start.36 = (s32[256]{0:T(256)S(1)}, s32[256]{0:T(256)}, u32[]{:S(2)}) copy-start(s32[256]{0:T(256)} %copy-done.34) | copy-start | bytes 3076
  662.3 44.7 %copy-start.40 = (f32[256]{0:T(256)S(1)}, f32[256]{0:T(256)}, u32[]{:S(2)}) copy-start(f32[256]{0:T(256)} %copy-done.39) | copy-start | bytes 3076
  662.3 44.7 %copy-start.44 = (f32[256]{0:T(256)S(1)}, f32[256]{0:T(256)}, u32[]{:S(2)}) copy-start(f32[256]{0:T(256)} %copy-done.43) | copy-start | bytes 3076
  672.5 92.6 %copy-start.15 = (f32[2,1]{0,1:T(1,128)S(1)}, f32[2,1]{0,1:T(1,128)}, u32[]{:S(2)}) copy-start(f32[2,1]{0,1:T(1,128)} %copy-done.14) | copy-start | bytes 28
  672.5 92.6 %copy-start.27 = (f32[2]{0:T(128)S(1)}, f32[2]{0:T(128)}, u32[]{:S(2)}) copy-start(f32[2]{0:T(128)} %copy-done.26) | copy-start | bytes 28
  672.5 92.6 %copy-start.19 = (f32[2,2]{0,1:T(2,128)S(1)}, f32[2,2]{0,1:T(2,128)}, u32[]{:S(2)}) copy-start(f32[2,2]{0,1:T(2,128)} %copy-done.18) | copy-start | bytes 52
  672.5 92.6 %copy-start.23 = (f32[2]{0:T(128)S(1)}, f32[2]{0:T(128)}, u32[]{:S(2)}) copy-start(f32[2]{0:T(128)} %copy-done.22) | copy-start | bytes 28
  672.5 92.6 %copy-start.31 = (f32[2]{0:T(128)S(1)}, f32[2]{0:T(128)}, u32[]{:S(2)}) copy-start(f32[2]{0:T(128)} %copy-done.30) | copy-start | bytes 28
  672.5 92.7 %copy-start.3 = (f32[2,2,64,256]{3,2,1,0:T(8,128)S(1)}, f32[2,2,64,256]{3,2,1,0:T(8,128)}, u32[]{:S(2)}) copy-start(f32[2,2,64,256]{3,2,1,0:T(8,128)} %param.3) | copy-start | bytes 786436
  679.8 86.9 %copy-start.6 = (f32[64]{0:T(128)S(1)}, f32[64]{0:T(128)}, u32[]{:S(2)}) copy-start(f32[64]{0:T(128)} %copy-done.4) | copy-start | bytes 772
  679.8 86.9 %copy-start.10 = (f32[64]{0:T(128)S(1)}, f32[64]{0:T(128)}, u32[]{:S(2)}) copy-start(f32[64]{0:T(128)} %copy-done.8) | copy-start | bytes 772
  765.4 182.2 %copy-start = (f32[2,2,64,256]{3,2,1,0:T(8,128)}, f32[2,2,64,256]{3,2,1,0:T(8,128)S(1)}, u32[]{:S(2)}) copy-start(f32[2,2,64,256]{3,2,1,0:T(8,128)S(1)} %multiply_add_fusion.9) | copy-start | bytes 786436
  845.3 44.2 %copy-start.33 = (f32[2,2,64,256]{3,2,1,0:T(8,128)S(1)}, f32[2,2,64,256]{3,2,1,0:T(8,128)}, u32[]{:S(2)}) copy-start(f32[2,2,64,256]{3,2,1,0:T(8,128)} %param.4) | copy-start | bytes 786436
  845.3 44.2 %copy-start.37 = (s32[256]{0:T(256)S(1)}, s32[256]{0:T(256)}, u32[]{:S(2)}) copy-start(s32[256]{0:T(256)} %copy-done.34) | copy-start | bytes 3076
  845.3 44.2 %copy-start.41 = (f32[256]{0:T(256)S(1)}, f32[256]{0:T(256)}, u32[]{:S(2)}) copy-start(f32[256]{0:T(256)} %copy-done.39) | copy-start | bytes 3076
  845.3 44.2 %copy-start.45 = (f32[256]{0:T(256)S(1)}, f32[256]{0:T(256)}, u32[]{:S(2)}) copy-start(f32[256]{0:T(256)} %copy-done.43) | copy-start | bytes 3076
  855.4 93.7 %copy-start.7 = (f32[64]{0:T(128)S(1)}, f32[64]{0:T(128)}, u32[]{:S(2)}) copy-start(f32[64]{0:T(128)} %copy-done.4) | copy-start | bytes 772
  855.4 93.7 %copy-start.11 = (f32[64]{0:T(128)S(1)}, f32[64]{0:T(128)}, u32[]{:S(2)}) copy-start(f32[64]{0:T(128)} %copy-done.8) | copy-start | bytes 772
  947.6 1.6 copy-start.28
  1124.5 1.6 copy-start.12
  1124.5 1.6 copy-start.24
  1324.9 1.6 copy-start.16
  1324.9 1.6 copy-start.20
  1421.9 44.4 %copy-start.38 = (s32[256]{0:T(256)S(1)}, s32[256]{0:T(256)}, u32[]{:S(2)}) copy-start(s32[256]{0:T(256)} %copy-done.34) | copy-start | bytes 3076
  1421.9 44.4 %copy-start.42 = (f32[256]{0:T(256)S(1)}, f32[256]{0:T(256)}, u32[]{:S(2)}) copy-start(f32[256]{0:T(256)} %copy-done.39) | copy-start | bytes 3076
  1421.9 44.4 %copy-start.46 = (f32[256]{0:T(256)S(1)}, f32[256]{0:T(256)}, u32[]{:S(2)}) copy-start(f32[256]{0:T(256)} %copy-done.43) | copy-start | bytes 3076
  1432.2 92.2 %copy-start.13 = (f32[2,1]{0,1:T(1,128)S(1)}, f32[2,1]{0,1:T(1,128)}, u32[]{:S(2)}) copy-start(f32[2,1]{0,1:T(1,128)} %copy-done.12) | copy-start | bytes 28
  1432.2 92.2 %copy-start.25 = (f32[2]{0:T(128)S(1)}, f32[2]{0:T(128)}, u32[]{:S(2)}) copy-start(f32[2]{0:T(128)} %copy-done.24) | copy-start | bytes 28
  1432.2 92.2 %copy-start.17 = (f32[2,2]{0,1:T(2,128)S(1)}, f32[2,2]{0,1:T(2,128)}, u32[]{:S(2)}) copy-start(f32[2,2]{0,1:T(2,128)} %copy-done.16) | copy-start | bytes 52
  1432.2 92.2 %copy-start.21 = (f32[2]{0:T(128)S(1)}, f32[2]{0:T(128)}, u32[]{:S(2)}) copy-start(f32[2]{0:T(128)} %copy-done.20) | copy-start | bytes 28
  1432.2 92.2 %copy-start.29 = (f32[2]{0:T(128)S(1)}, f32[2]{0:T(128)}, u32[]{:S(2)}) copy-start(f32[2]{0:T(128)} %copy-done.28) | copy-start | bytes 28
  1432.2 92.3 %copy-start.1 = (f32[2,2,64,256]{3,2,1,0:T(8,128)S(1)}, f32[2,2,64,256]{3,2,1,0:T(8,128)}, u32[]{:S(2)}) copy-start(f32[2,2,64,256]{3,2,1,0:T(8,128)} %copy-done) | copy-start | bytes 786436
